TPU v7x, 32 devices: a whole 2x2x4 slice. The times are simulated.
32 devices in a mesh: section: 2 (over x), dp: 8 (over z, y), mp: 2 (over core).
Axes of the slice: x: 2, y: 2, z: 4, core: 2. Of those that a mesh axis runs over, the one named last changes fastest.
Arguments:
- layer_inputs: bfloat16 [2, 128, 4096], P('section', None, 'mp'), may hold values from -6 to 6
- pre_act: bfloat16 [2, 128, 8192], P('section', None, 'dp'), may hold values from -6 to 6
- out_grad: bfloat16 [128, 4096], P(None, 'mp'), may hold values from -4 to 4
- w_in: bfloat16 [8, 2, 512, 4096], P('dp', 'section', None, 'mp'), may hold values from -0.09375 to 0.09375
- w_out: bfloat16 [8, 2, 512, 4096], P('dp', 'section', None, 'mp'), may hold values from -0.0625 to 0.0625
Outputs:
- in_grads: bfloat16 [2, 128, 4096], P('section', None, 'mp')
- grad_in: float32 [8, 2, 512, 4096], P('dp', 'section', None, 'mp')
- grad_out: float32 [8, 2, 512, 4096], P('dp', 'section', None, 'mp')
All inputs are finite; a program needn't handle non-finite values.
Results may differ from a plain program's by a relative error of at most 0.035.
Values may be sent and summed in bfloat16 or wider, within the bound.
A program may use at most 64 MiB of HBM per device.

v0:
```python
import jax
import jax.numpy as jnp
from jax import lax
from jax.sharding import PartitionSpec as P

MICRO = 2


def shifted(value, axis, by):
    size = lax.axis_size(axis)
    pairs = [(i, i + by) for i in range(size) if 0 <= i + by < size]
    return lax.ppermute(value, axis, pairs)


def gelu_slope(value):
    cdf = 0.5 * (1.0 + lax.erf(value * 0.7071067811865476))
    dens = jnp.exp(-0.5 * value * value) * 0.3989422804014327
    return cdf + value * dens


def rounded(value):
    return lax.optimization_barrier(value.astype(jnp.bfloat16)).astype(jnp.float32)


def by_tokens(left, right):
    return lax.dot_general(
        left, right, (((0,), (0,)), ((), ())), preferred_element_type=jnp.float32
    )


def body(layer_inputs, pre_act, out_grad, w_in, w_out):
    sections = lax.axis_size("section")
    spot = lax.axis_index("section")
    tok_rows = out_grad.shape[0]
    block = tok_rows // MICRO
    width = out_grad.shape[1]
    full_in, full_out = (
        lax.all_gather(w_in, "section", axis=1, tiled=True),
        lax.all_gather(w_out, "section", axis=1, tiled=True),
    )
    units = full_in.shape[1] * full_in.shape[2]
    per_block = full_in.shape[2]
    in_rows = full_in.reshape(units, width)
    out_rows = full_out.reshape(units, width)
    inputs = layer_inputs[0]
    saved = pre_act[0]
    is_last = spot == sections - 1

    def advance(step, state):
        incoming, dys, gees, results = state
        micro_id = step - (sections - 1 - spot)
        valid = jnp.logical_and(micro_id >= 0, micro_id < MICRO)
        begin = jnp.clip(micro_id, 0, MICRO - 1) * block
        given = lax.dynamic_slice_in_dim(out_grad, begin, block, 0)
        upper = jnp.where(is_last, given, incoming)
        partial_value = lax.dot_general(
            upper, out_rows, (((1,), (1,)), ((), ())), preferred_element_type=jnp.float32
        )
        summed = lax.psum(partial_value.astype(jnp.bfloat16), "mp").astype(jnp.float32)
        rows_pre = lax.dynamic_slice_in_dim(saved, begin, block, 0).astype(jnp.float32)
        gee = (summed * gelu_slope(rows_pre)).astype(jnp.bfloat16)
        branch = jnp.dot(gee, in_rows, preferred_element_type=jnp.float32)
        total = lax.psum(branch.astype(jnp.bfloat16), "dp").astype(jnp.float32)
        result = (upper.astype(jnp.float32) + total).astype(jnp.bfloat16)
        outgoing = shifted(result, "section", -1)
        old_dy = lax.dynamic_slice_in_dim(dys, begin, block, 0)
        old_gee = lax.dynamic_slice_in_dim(gees, begin, block, 0)
        old_res = lax.dynamic_slice_in_dim(results, begin, block, 0)
        dys = lax.dynamic_update_slice_in_dim(dys, jnp.where(valid, upper, old_dy), begin, 0)
        gees = lax.dynamic_update_slice_in_dim(gees, jnp.where(valid, gee, old_gee), begin, 0)
        results = lax.dynamic_update_slice_in_dim(
            results, jnp.where(valid, result, old_res), begin, 0
        )
        return (outgoing, dys, gees, results)

    start_state = (
        jnp.zeros((block, width), jnp.bfloat16),
        jnp.zeros((tok_rows, width), jnp.bfloat16),
        jnp.zeros((tok_rows, units), jnp.bfloat16),
        jnp.zeros((tok_rows, width), jnp.bfloat16),
    )
    final_state = lax.fori_loop(0, sections + MICRO - 1, advance, start_state)
    dys = final_state[1]
    gees = final_state[2]
    results = final_state[3]
    hidden = jax.nn.gelu(saved.astype(jnp.float32), approximate=False).astype(jnp.bfloat16)
    offset = spot * per_block
    empty = jnp.zeros((per_block, width), jnp.float32)
    piece = (
        lax.all_gather(inputs[None], "section", axis=0, tiled=True),
        lax.all_gather(dys[None], "section", axis=0, tiled=True),
        lax.all_gather(gees[None], "section", axis=0, tiled=True),
        lax.all_gather(hidden[None], "section", axis=0, tiled=True),
    )
    acc_in = empty
    acc_out = empty
    for row in range(piece[0].shape[0]):
        gee_cols = lax.dynamic_slice_in_dim(piece[2][row], offset, per_block, 1)
        hid_cols = lax.dynamic_slice_in_dim(piece[3][row], offset, per_block, 1)
        acc_in = acc_in + rounded(by_tokens(gee_cols, piece[0][row]))
        acc_out = acc_out + rounded(by_tokens(hid_cols, piece[1][row]))
    acc_in, acc_out = (acc_in, acc_out)
    grad_in = acc_in.reshape(1, 1, per_block, width)
    grad_out = acc_out.reshape(1, 1, per_block, width)
    return (results[None], grad_in, grad_out)


def solution(mesh):
    in_specs = (
        P("section", None, "mp"),
        P("section", None, "dp"),
        P(None, "mp"),
        P("dp", "section", None, "mp"),
        P("dp", "section", None, "mp"),
    )
    out_specs = (
        P("section", None, "mp"),
        P("dp", "section", None, "mp"),
        P("dp", "section", None, "mp"),
    )
    return jax.shard_map(body, mesh=mesh, in_specs=in_specs, out_specs=out_specs, check_vma=False)
```

profile of v0, /device:TPU:0, one launch (start us, length us, event | category | flops | bytes accessed | tf_op | source)
XLA Modules:
  0.0 509.6 jit_solution(17135875296356808804)
XLA Ops:
  7.2 0.0 copy-start.4
  7.2 0.0 copy-start.2
  7.2 0.0 all-gather.7.cloned.1.call-start
  7.2 0.7 all-gather.7.cloned.1.call-update
  7.9 0.0 all-gather.9.cloned.1.call-start
  8.0 0.7 all-gather.9.cloned.1.call-update
  8.7 60.3 %all-gather.7.cloned.1.call-done = bf16[1,2,512,2048]{3,2,0,1:T(8,128)(2,1)} async-done(((bf16[1,1,512,2048]{3,2,0,1:T(8,128)(2,1)}), bf16[1,2,512,2048]{3,2,0,1:T(8,128)(2,1)}) %all-gather.7.cloned.1.call-update) | async-done | bytes 4194320 | tf_op jit(solution)/shard_map/all_gather | solution.py:39
  69.0 58.3 %all-gather.9.cloned.1.call-done = bf16[1,2,512,2048]{3,2,0,1:T(8,128)(2,1)} async-done(((bf16[1,1,512,2048]{3,2,0,1:T(8,128)(2,1)}), bf16[1,2,512,2048]{3,2,0,1:T(8,128)(2,1)}) %all-gather.9.cloned.1.call-update) | async-done | bytes 4194320 | tf_op jit(solution)/shard_map/all_gather | solution.py:38
  127.5 0.0 copy-done.4
  127.5 0.0 copy-done.2
  127.5 320.8 %while.21 = (s32[]{:T(128)}, bf16[64,2048]{1,0:T(8,128)(2,1)S(1)}, bf16[128,2048]{1,0:T(8,128)(2,1)S(1)}, bf16[128,1024]{1,0:T(8,128)(2,1)S(1)}, bf16[128,2048]{...) while((s32[]{:T(128)}, bf16[64,2048]{1,0:T(8,128)(2,1)S(1)}, ...), condition=%wide.region_3.4_spmd, body=%wide.region_0.3_spmd.sunk | while | flops 539820032 | bytes 16384420 | solution.py:82
  127.5 0.0 all-reduce.3.cloned.1.call-start
  127.6 0.1 select_dynamic-update-slice_fusion.6
  127.7 4.2 convolution_convert_fusion.8
  131.9 0.0 all-reduce.3.cloned.1.call-update
  132.0 0.0 all-reduce.5.cloned.1.call-start
  132.0 18.0 %all-reduce.3.cloned.1.call-done = bf16[64,1024]{1,0:T(8,128)(2,1)} async-done(((bf16[64,1024]{1,0:T(8,128)(2,1)}), bf16[64,1024]{1,0:T(8,128)(2,1)}) %all-reduce.3.cloned.1.call-update) | async-done | bytes 131088 | tf_op jit(solution)/shard_map/while/body/eval_jaxpr/psum | solution.py:59
  150.0 3.9 convolution_convert_fusion.9
  153.9 0.0 all-reduce.5.cloned.1.call-update
  153.9 72.4 %all-reduce.5.cloned.1.call-done = bf16[64,2048]{1,0:T(8,128)(2,1)} async-done(((bf16[64,2048]{1,0:T(8,128)(2,1)}), bf16[64,2048]{1,0:T(8,128)(2,1)}) %all-reduce.5.cloned.1.call-update) | async-done | bytes 262160 | tf_op jit(solution)/shard_map/while/body/eval_jaxpr/psum | solution.py:63
  226.3 1.1 select_dynamic-update-slice_fusion.7
  227.3 1.3 collective-permute-start
  228.6 0.0 copy-done
  228.7 0.2 select_dynamic-update-slice_fusion.8
  228.8 6.8 %collective-permute-done = bf16[64,2048]{1,0:T(8,128)(2,1)S(1)} collective-permute-done((bf16[64,2048]{1,0:T(8,128)(2,1)S(1)}, bf16[64,2048]{1,0:T(8,128)(2,1)S(1)}, u32[]{:S(2)}, u32[]{:S(2)}) %collective-permute-start) | collective-permute-done | bytes 262176 | tf_op jit(solution)/shard_map/while/body/eval_jaxpr/ppermute | solution.py:12
  235.6 0.1 select_dynamic-update-slice_fusion.6
  235.7 4.2 convolution_convert_fusion.8
  240.0 0.0 all-reduce.3.cloned.1.call-update
  240.0 0.0 all-reduce.5.cloned.1.call-start
  240.1 16.3 %all-reduce.3.cloned.1.call-done = bf16[64,1024]{1,0:T(8,128)(2,1)} async-done(((bf16[64,1024]{1,0:T(8,128)(2,1)}), bf16[64,1024]{1,0:T(8,128)(2,1)}) %all-reduce.3.cloned.1.call-update) | async-done | bytes 131088 | tf_op jit(solution)/shard_map/while/body/eval_jaxpr/psum | solution.py:59
  256.4 3.9 convolution_convert_fusion.9
  260.2 0.0 all-reduce.5.cloned.1.call-update
  260.3 72.4 %all-reduce.5.cloned.1.call-done = bf16[64,2048]{1,0:T(8,128)(2,1)} async-done(((bf16[64,2048]{1,0:T(8,128)(2,1)}), bf16[64,2048]{1,0:T(8,128)(2,1)}) %all-reduce.5.cloned.1.call-update) | async-done | bytes 262160 | tf_op jit(solution)/shard_map/while/body/eval_jaxpr/psum | solution.py:63
  332.6 1.1 select_dynamic-update-slice_fusion.7
  333.7 1.3 collective-permute-start
  335.0 0.2 select_dynamic-update-slice_fusion.8
  335.2 6.8 %collective-permute-done = bf16[64,2048]{1,0:T(8,128)(2,1)S(1)} collective-permute-done((bf16[64,2048]{1,0:T(8,128)(2,1)S(1)}, bf16[64,2048]{1,0:T(8,128)(2,1)S(1)}, u32[]{:S(2)}, u32[]{:S(2)}) %collective-permute-start) | collective-permute-done | bytes 262176 | tf_op jit(solution)/shard_map/while/body/eval_jaxpr/ppermute | solution.py:12
  342.0 0.0 all-reduce.3.cloned.1.call-start
  342.0 0.1 select_dynamic-update-slice_fusion.6
  342.1 4.2 convolution_convert_fusion.8
  346.4 0.0 all-reduce.3.cloned.1.call-update
  346.4 0.0 all-reduce.5.cloned.1.call-start
  346.4 16.3 %all-reduce.3.cloned.1.call-done = bf16[64,1024]{1,0:T(8,128)(2,1)} async-done(((bf16[64,1024]{1,0:T(8,128)(2,1)}), bf16[64,1024]{1,0:T(8,128)(2,1)}) %all-reduce.3.cloned.1.call-update) | async-done | bytes 131088 | tf_op jit(solution)/shard_map/while/body/eval_jaxpr/psum | solution.py:59
  362.7 3.9 convolution_convert_fusion.9
  366.6 0.0 all-reduce.5.cloned.1.call-update
  366.6 72.4 %all-reduce.5.cloned.1.call-done = bf16[64,2048]{1,0:T(8,128)(2,1)} async-done(((bf16[64,2048]{1,0:T(8,128)(2,1)}), bf16[64,2048]{1,0:T(8,128)(2,1)}) %all-reduce.5.cloned.1.call-update) | async-done | bytes 262160 | tf_op jit(solution)/shard_map/while/body/eval_jaxpr/psum | solution.py:63
  439.0 1.1 select_dynamic-update-slice_fusion.7
  440.1 1.3 collective-permute-start
  441.4 0.2 select_dynamic-update-slice_fusion.8
  441.5 6.8 %collective-permute-done = bf16[64,2048]{1,0:T(8,128)(2,1)S(1)} collective-permute-done((bf16[64,2048]{1,0:T(8,128)(2,1)S(1)}, bf16[64,2048]{1,0:T(8,128)(2,1)S(1)}, u32[]{:S(2)}, u32[]{:S(2)}) %collective-permute-start) | collective-permute-done | bytes 262176 | tf_op jit(solution)/shard_map/while/body/eval_jaxpr/ppermute | solution.py:12
  448.3 0.7 all-gather.11.cloned.1.call-update
  449.1 0.0 all-gather.13.cloned.1.call-start
  449.1 1.1 fusion.10
  450.2 8.1 %all_gather.22 = bf16[2,128,1024]{2,1,0:T(8,128)(2,1)S(1)} all-gather(bf16[1,128,1024]{2,1,0:T(8,128)(2,1)S(1)} %fusion.10), channel_id=1, replica_groups=mesh['section'=2,'dp'=8,'mp'=2] {'section'}, dimensions={0}, use_global_device_ids=true | all-gather | bytes 786432 | tf_op jit(solution)/shard_map/all_gather | solution.py:93
  458.3 12.7 %all-gather = bf16[256,1024]{1,0:T(8,128)(2,1)S(1)} all-gather(bf16[128,1024]{1,0:T(8,128)(2,1)S(1)} %get-tuple-element.260), channel_id=2, replica_groups=mesh['section'=2,'dp'=8,'mp'=2] {'section'}, dimensions={0}, use_global_device_ids=true | all-gather | bytes 786432 | tf_op jit(solution)/shard_map/all_gather | solution.py:92
  471.0 0.0 all-gather.13.cloned.1.call-update
  471.1 3.3 all-gather.11.cloned.1.call-done
  474.4 1.8 convolution_convert_fusion.4
  476.2 1.8 convolution_convert_fusion.5
  478.0 2.8 add_bitcast_fusion.1
  480.8 15.6 %all-gather.13.cloned.1.call-done = bf16[256,2048]{1,0:T(8,128)(2,1)} async-done(((bf16[128,2048]{1,0:T(8,128)(2,1)}), bf16[256,2048]{1,0:T(8,128)(2,1)}) %all-gather.13.cloned.1.call-update) | async-done | bytes 1048592 | tf_op jit(solution)/shard_map/all_gather | solution.py:91
  496.4 1.8 convolution_convert_fusion.2
  498.1 1.8 convolution_convert_fusion.3
  499.9 2.8 add_bitcast_fusion
  (17 shorter events, 0.2 us)
Async XLA Ops:
  7.2 120.3 %copy-start.4 = (bf16[128,2048]{1,0:T(8,128)(2,1)S(1)}, bf16[128,2048]{1,0:T(8,128)(2,1)}, u32[]{:S(2)}) copy-start(bf16[128,2048]{1,0:T(8,128)(2,1)} %param.9) | copy-start | bytes 1572868
  7.2 120.3 %copy-start.2 = (bf16[1,128,1024]{2,1,0:T(8,128)(2,1)S(1)}, bf16[1,128,1024]{2,1,0:T(8,128)(2,1)}, u32[]{:S(2)}) copy-start(bf16[1,128,1024]{2,1,0:T(8,128)(2,1)} %param.8) | copy-start | bytes 786436
  7.2 61.8 %all-gather.7.cloned.1.call-start = ((), (), s32[]{:S(2)}) async-start(), calls=%async_computation | async-start | bytes 6291456 | tf_op jit(solution)/shard_map/all_gather | solution.py:39
  7.9 119.4 %all-gather.9.cloned.1.call-start = ((), (), s32[]{:S(2)}) async-start(), calls=%async_computation.1 | async-start | bytes 6291456 | tf_op jit(solution)/shard_map/all_gather | solution.py:38
  127.5 22.5 %all-reduce.3.cloned.1.call-start = ((), (), s32[]{:S(2)}) async-start(), calls=%async_computation.4 | async-start | bytes 262144 | tf_op jit(solution)/shard_map/while/body/eval_jaxpr/psum | solution.py:59
  132.0 94.3 %all-reduce.5.cloned.1.call-start = ((), (), s32[]{:S(2)}) async-start(), calls=%async_computation.5 | async-start | bytes 524288 | tf_op jit(solution)/shard_map/while/body/eval_jaxpr/psum | solution.py:63
  150.0 78.6 %copy-start = (bf16[64,1024]{1,0:T(8,128)(2,1)S(1)}, bf16[64,1024]{1,0:T(8,128)(2,1)}, u32[]{:S(2)}) copy-start(bf16[64,1024]{1,0:T(8,128)(2,1)} %all-reduce.3.cloned.1.call-done) | copy-start | bytes 393220 | tf_op jit(solution)/shard_map/while
  227.3 8.3 %collective-permute-start = (bf16[64,2048]{1,0:T(8,128)(2,1)S(1)}, bf16[64,2048]{1,0:T(8,128)(2,1)S(1)}, u32[]{:S(2)}, u32[]{:S(2)}) collective-permute-start(bf16[64,2048]{1,0:T(8,128)(2,1)S(1)} %get-tuple-element.364), channel_id=1, source_target_pairs={{16,0},{17,1},{18,2},{19,3},{20,4},{21,5},{22,6},{23,7},{24,8},{25... | collective-permute-start | bytes 786440 | tf_op jit(solution)/shard_map/while/body/eval_jaxpr/ppermute | solution.py:12
  235.6 20.8 %all-reduce.3.cloned.1.call-start = ((), (), s32[]{:S(2)}) async-start(), calls=%async_computation.4 | async-start | bytes 262144 | tf_op jit(solution)/shard_map/while/body/eval_jaxpr/psum | solution.py:59
  240.0 92.6 %all-reduce.5.cloned.1.call-start = ((), (), s32[]{:S(2)}) async-start(), calls=%async_computation.5 | async-start | bytes 524288 | tf_op jit(solution)/shard_map/while/body/eval_jaxpr/psum | solution.py:63
  256.4 78.6 %copy-start = (bf16[64,1024]{1,0:T(8,128)(2,1)S(1)}, bf16[64,1024]{1,0:T(8,128)(2,1)}, u32[]{:S(2)}) copy-start(bf16[64,1024]{1,0:T(8,128)(2,1)} %all-reduce.3.cloned.1.call-done) | copy-start | bytes 393220 | tf_op jit(solution)/shard_map/while
  333.7 8.3 %collective-permute-start = (bf16[64,2048]{1,0:T(8,128)(2,1)S(1)}, bf16[64,2048]{1,0:T(8,128)(2,1)S(1)}, u32[]{:S(2)}, u32[]{:S(2)}) collective-permute-start(bf16[64,2048]{1,0:T(8,128)(2,1)S(1)} %get-tuple-element.364), channel_id=1, source_target_pairs={{16,0},{17,1},{18,2},{19,3},{20,4},{21,5},{22,6},{23,7},{24,8},{25... | collective-permute-start | bytes 786440 | tf_op jit(solution)/shard_map/while/body/eval_jaxpr/ppermute | solution.py:12
  342.0 20.8 %all-reduce.3.cloned.1.call-start = ((), (), s32[]{:S(2)}) async-start(), calls=%async_computation.4 | async-start | bytes 262144 | tf_op jit(solution)/shard_map/while/body/eval_jaxpr/psum | solution.py:59
  346.4 92.6 %all-reduce.5.cloned.1.call-start = ((), (), s32[]{:S(2)}) async-start(), calls=%async_computation.5 | async-start | bytes 524288 | tf_op jit(solution)/shard_map/while/body/eval_jaxpr/psum | solution.py:63
  362.7 78.6 %copy-start = (bf16[64,1024]{1,0:T(8,128)(2,1)S(1)}, bf16[64,1024]{1,0:T(8,128)(2,1)}, u32[]{:S(2)}) copy-start(bf16[64,1024]{1,0:T(8,128)(2,1)} %all-reduce.3.cloned.1.call-done) | copy-start | bytes 393220 | tf_op jit(solution)/shard_map/while
  440.1 8.3 %collective-permute-start = (bf16[64,2048]{1,0:T(8,128)(2,1)S(1)}, bf16[64,2048]{1,0:T(8,128)(2,1)S(1)}, u32[]{:S(2)}, u32[]{:S(2)}) collective-permute-start(bf16[64,2048]{1,0:T(8,128)(2,1)S(1)} %get-tuple-element.364), channel_id=1, source_target_pairs={{16,0},{17,1},{18,2},{19,3},{20,4},{21,5},{22,6},{23,7},{24,8},{25... | collective-permute-start | bytes 786440 | tf_op jit(solution)/shard_map/while/body/eval_jaxpr/ppermute | solution.py:12
  448.3 22.7 %copy-start.1 = (bf16[128,2048]{1,0:T(8,128)(2,1)}, bf16[128,2048]{1,0:T(8,128)(2,1)S(1)}, u32[]{:S(2)}) copy-start(bf16[128,2048]{1,0:T(8,128)(2,1)S(1)} %get-tuple-element.261) | copy-start | bytes 1572868
  448.3 29.6 %copy-start.3 = (bf16[128,2048]{1,0:T(8,128)(2,1)}, bf16[128,2048]{1,0:T(8,128)(2,1)S(1)}, u32[]{:S(2)}) copy-start(bf16[128,2048]{1,0:T(8,128)(2,1)S(1)} %get-tuple-element.259) | copy-start | bytes 1572868
  448.3 26.1 %all-gather.11.cloned.1.call-start = ((), (), s32[]{:S(2)}) async-start(), calls=%async_computation.2 | async-start | bytes 1572864 | tf_op jit(solution)/shard_map/all_gather | solution.py:90
  449.1 47.3 %all-gather.13.cloned.1.call-start = ((), (), s32[]{:S(2)}) async-start(), calls=%async_computation.3 | async-start | bytes 1572864 | tf_op jit(solution)/shard_map/all_gather | solution.py:91
Sparse Core Ops, SparseCore 0:
  9.5 59.4 all-gather.6
  70.6 56.7 all-gather.8
  132.1 17.8 all-reduce.2
  154.0 72.1 all-reduce.4
  240.1 16.1 all-reduce.2
  260.4 72.2 all-reduce.4
  346.5 16.1 all-reduce.2
  366.7 72.2 all-reduce.4
  450.7 23.6 all-gather.10
  476.4 19.9 all-gather.12
where the time goes:
time: 510 us
  waiting for transfers between devices  428 us (84%)
  matrix products  31.4 us (6%)
  blocking collectives  20.7 us (4%)
  between operations  14.2 us (3%)
  other arithmetic  10.8 us (2%)
    psum x3, waiting for transfers between devices, advance(): total = lax.psum(branch.astype(jnp.bfloat16), 'dp').astype(jnp.float32)  217 us
    all_gather x1, waiting for transfers between devices, body(): lax.all_gather(w_out, 'section', axis=1, tiled=True)  60.3 us
    all_gather x1, waiting for transfers between devices, body(): lax.all_gather(w_in, 'section', axis=1, tiled=True)  58.3 us
    psum x3, waiting for transfers between devices, advance(): lax.psum(partial_value.astype(jnp.bfloat16), 'mp').astype(jnp.float32)  50.6 us
    ppermute x3, waiting for transfers between devices, shifted(): return lax.ppermute(value, axis, pairs)  20.4 us
    all_gather x1, waiting for transfers between devices, body(): lax.all_gather(dys[None], 'section', axis=0, tiled=True)  15.6 us
    dot_general x3, matrix products, advance(): lax.dot_general(upper, out_rows, (((1,), (1,)), ((), ())), preferred_elem...  12.7 us
    all_gather x1, blocking collectives, body(): lax.all_gather(gees[None], 'section', axis=0, tiled=True)  12.7 us
  transfers between devices with their start and end apart: 13, of which 13 were waited for; matrix products, arithmetic and copies ran while one was open for 2% of the time, Pallas kernels for 0%

commit v1 on v0

--- a/solution.py
+++ b/solution.py
@@ -1,9 +1,42 @@
+import functools
 import jax
 import jax.numpy as jnp
 from jax import lax
 from jax.sharding import PartitionSpec as P
 
 MICRO = 2
+
+
+def mix_flows(original, along_dim):
+    original = jnp.moveaxis(original, 0, along_dim)
+    d_next = original.shape
+    plain = original.reshape(
+        *d_next[:along_dim], d_next[along_dim] * d_next[along_dim + 1], *d_next[along_dim + 2 :]
+    )
+    return plain
+
+
+def _use_rings(x_local, which_axis):
+    aux, wide_out = (lax.axis_size(which_axis), lax.axis_index(which_axis))
+    answer, kept_arr = (x_local[None], 1)
+    while kept_arr < aux:
+        view_out = lax.ppermute(
+            answer, axis_name=which_axis, perm=list(map(lambda k: (k, k ^ kept_arr), range(aux)))
+        )
+        current_value = wide_out & kept_arr == 0
+        answer = jnp.concatenate(
+            [jnp.where(current_value, answer, view_out), jnp.where(current_value, view_out, answer)]
+        )
+        kept_arr *= 2
+    return answer
+
+
+def mark_plate(block_in, matrix, ndim_at):
+    k_now = mix_flows(_use_rings(block_in, matrix), ndim_at)
+    return k_now
+
+
+switch_files = functools.partial(mark_plate, matrix="section", ndim_at=1)
 
 
 def shifted(value, axis, by):
@@ -34,10 +67,7 @@
     tok_rows = out_grad.shape[0]
     block = tok_rows // MICRO
     width = out_grad.shape[1]
-    full_in, full_out = (
-        lax.all_gather(w_in, "section", axis=1, tiled=True),
-        lax.all_gather(w_out, "section", axis=1, tiled=True),
-    )
+    full_in, full_out = (switch_files(w_in), lax.all_gather(w_out, "section", axis=1, tiled=True))
     units = full_in.shape[1] * full_in.shape[2]
     per_block = full_in.shape[2]
     in_rows = full_in.reshape(units, width)

time: 510 us -> 486 us (0.953)
  waiting for transfers between devices: 428 us -> 397 us
    ppermute x0 -> x1, waiting for transfers between devices: none -> 80.7 us  [_use_rings(): lax.ppermute(answer, axis_name=which_axis, perm=list(map(lambda k: (k, k...]
    all_gather x1 -> x0, waiting for transfers between devices: 58.3 us -> none  [body(): lax.all_gather(w_in, 'section', axis=1, tiled=True)]
    all_gather x1, waiting for transfers between devices: 60.3 us -> 6.07 us  [body(): lax.all_gather(w_out, 'section', axis=1, tiled=True)]
  transfers between devices with their start and end apart: 13 -> 13, of which waited for: 13 -> 13; matrix products, arithmetic and copies ran while one was open for 2% -> 3% of each run, Pallas kernels for 0% -> 0%
where the time goes in v1:
time: 486 us
  waiting for transfers between devices  397 us (82%)
  matrix products  31.4 us (6%)
  blocking collectives  20.7 us (4%)
  other arithmetic  15 us (3%)
  between operations  13.9 us (3%)
  starting transfers between devices  7.17 us (1%)
    psum x3, waiting for transfers between devices, advance(): total = lax.psum(branch.astype(jnp.bfloat16), 'dp').astype(jnp.float32)  217 us
    ppermute x1, waiting for transfers between devices, _use_rings(): lax.ppermute(answer, axis_name=which_axis, perm=list(map(lambda k: (k, k...  80.7 us
    psum x3, waiting for transfers between devices, advance(): lax.psum(partial_value.astype(jnp.bfloat16), 'mp').astype(jnp.float32)  52.1 us
    ppermute x3, waiting for transfers between devices, shifted(): return lax.ppermute(value, axis, pairs)  20.4 us
    all_gather x1, waiting for transfers between devices, body(): lax.all_gather(dys[None], 'section', axis=0, tiled=True)  15.7 us
    dot_general x3, matrix products, advance(): lax.dot_general(upper, out_rows, (((1,), (1,)), ((), ())), preferred_elem...  12.7 us
    all_gather x1, blocking collectives, body(): lax.all_gather(gees[None], 'section', axis=0, tiled=True)  12.7 us
    dot_general x3, matrix products, advance(): branch = jnp.dot(gee, in_rows, preferred_element_type=jnp.float32)  11.6 us
  transfers between devices with their start and end apart: 13, of which 13 were waited for; matrix products, arithmetic and copies ran while one was open for 3% of the time, Pallas kernels for 0%

profile of v1, /device:TPU:0, one launch (start us, length us, event | category | flops | bytes accessed | tf_op | source)
XLA Modules:
  0.0 485.6 jit_solution(8040776396674954654)
XLA Ops:
  7.2 0.0 all-gather.6.cloned.1.call-start
  7.2 0.7 all-gather.6.cloned.1.call-update
  7.9 3.0 collective-permute-start.1
  10.9 80.7 %collective-permute-done.1 = bf16[1,1,1,512,2048]{4,3,2,1,0:T(8,128)(2,1)S(1)} collective-permute-done((bf16[1,1,1,512,2048]{4,3,2,1,0:T(8,128)(2,1)}, bf16[1,1,1,512,2048]{4,3,2,1,0:T(8,128)(2,1)S(1)}, u32[]{:S(2)}, u32[]{:S(2)}) %collective-permute-start.1) | collective-permute-done | bytes 2097184 | tf_op jit(solution)/shard_map/ppermute | solution.py:23
  91.6 1.9 broadcast_select_fusion.1
  93.5 0.0 copy-start.2
  93.5 0.0 copy-start.4
  93.5 2.4 pad_maximum_fusion
  95.9 6.1 %all-gather.6.cloned.1.call-done = bf16[1,2,512,2048]{3,2,0,1:T(8,128)(2,1)} async-done(((bf16[1,1,512,2048]{3,2,0,1:T(8,128)(2,1)}), bf16[1,2,512,2048]{3,2,0,1:T(8,128)(2,1)}) %all-gather.6.cloned.1.call-update) | async-done | bytes 4194320 | tf_op jit(solution)/shard_map/all_gather | solution.py:70
  102.1 0.0 copy-done.2
  102.1 0.0 copy-done.4
  102.1 322.3 %while.21 = (s32[]{:T(128)}, bf16[64,2048]{1,0:T(8,128)(2,1)S(1)}, bf16[128,2048]{1,0:T(8,128)(2,1)S(1)}, bf16[128,1024]{1,0:T(8,128)(2,1)S(1)}, bf16[128,2048]{...) while((s32[]{:T(128)}, bf16[64,2048]{1,0:T(8,128)(2,1)S(1)}, ...), condition=%wide.region_3.4_spmd, body=%wide.region_0.3_spmd.sunk | while | flops 539820032 | bytes 16384420 | solution.py:112
  102.2 0.0 all-reduce.3.cloned.1.call-start
  102.2 0.1 select_dynamic-update-slice_fusion.6
  102.4 4.2 convolution_convert_fusion.8
  106.6 0.0 all-reduce.3.cloned.1.call-update
  106.6 0.0 all-reduce.5.cloned.1.call-start
  106.7 19.5 %all-reduce.3.cloned.1.call-done = bf16[64,1024]{1,0:T(8,128)(2,1)} async-done(((bf16[64,1024]{1,0:T(8,128)(2,1)}), bf16[64,1024]{1,0:T(8,128)(2,1)}) %all-reduce.3.cloned.1.call-update) | async-done | bytes 131088 | tf_op jit(solution)/shard_map/while/body/eval_jaxpr/psum | solution.py:89
  126.2 3.9 convolution_convert_fusion.9
  130.1 0.0 all-reduce.5.cloned.1.call-update
  130.1 72.4 %all-reduce.5.cloned.1.call-done = bf16[64,2048]{1,0:T(8,128)(2,1)} async-done(((bf16[64,2048]{1,0:T(8,128)(2,1)}), bf16[64,2048]{1,0:T(8,128)(2,1)}) %all-reduce.5.cloned.1.call-update) | async-done | bytes 262160 | tf_op jit(solution)/shard_map/while/body/eval_jaxpr/psum | solution.py:93
  202.4 1.1 select_dynamic-update-slice_fusion.7
  203.5 1.3 collective-permute-start
  204.8 0.0 copy-done
  204.8 0.2 select_dynamic-update-slice_fusion.8
  205.0 6.8 %collective-permute-done = bf16[64,2048]{1,0:T(8,128)(2,1)S(1)} collective-permute-done((bf16[64,2048]{1,0:T(8,128)(2,1)S(1)}, bf16[64,2048]{1,0:T(8,128)(2,1)S(1)}, u32[]{:S(2)}, u32[]{:S(2)}) %collective-permute-start) | collective-permute-done | bytes 262176 | tf_op jit(solution)/shard_map/while/body/eval_jaxpr/ppermute | solution.py:45
  211.8 0.1 select_dynamic-update-slice_fusion.6
  211.9 4.2 convolution_convert_fusion.8
  216.2 0.0 all-reduce.3.cloned.1.call-update
  216.2 0.0 all-reduce.5.cloned.1.call-start
  216.2 16.3 %all-reduce.3.cloned.1.call-done = bf16[64,1024]{1,0:T(8,128)(2,1)} async-done(((bf16[64,1024]{1,0:T(8,128)(2,1)}), bf16[64,1024]{1,0:T(8,128)(2,1)}) %all-reduce.3.cloned.1.call-update) | async-done | bytes 131088 | tf_op jit(solution)/shard_map/while/body/eval_jaxpr/psum | solution.py:89
  232.5 3.9 convolution_convert_fusion.9
  236.4 0.0 all-reduce.5.cloned.1.call-update
  236.4 72.4 %all-reduce.5.cloned.1.call-done = bf16[64,2048]{1,0:T(8,128)(2,1)} async-done(((bf16[64,2048]{1,0:T(8,128)(2,1)}), bf16[64,2048]{1,0:T(8,128)(2,1)}) %all-reduce.5.cloned.1.call-update) | async-done | bytes 262160 | tf_op jit(solution)/shard_map/while/body/eval_jaxpr/psum | solution.py:93
  308.8 1.1 select_dynamic-update-slice_fusion.7
  309.8 1.3 collective-permute-start
  311.2 0.2 select_dynamic-update-slice_fusion.8
  311.3 6.8 %collective-permute-done = bf16[64,2048]{1,0:T(8,128)(2,1)S(1)} collective-permute-done((bf16[64,2048]{1,0:T(8,128)(2,1)S(1)}, bf16[64,2048]{1,0:T(8,128)(2,1)S(1)}, u32[]{:S(2)}, u32[]{:S(2)}) %collective-permute-start) | collective-permute-done | bytes 262176 | tf_op jit(solution)/shard_map/while/body/eval_jaxpr/ppermute | solution.py:45
  318.1 0.1 select_dynamic-update-slice_fusion.6
  318.2 4.2 convolution_convert_fusion.8
  322.5 0.0 all-reduce.3.cloned.1.call-update
  322.5 0.0 all-reduce.5.cloned.1.call-start
  322.6 16.3 %all-reduce.3.cloned.1.call-done = bf16[64,1024]{1,0:T(8,128)(2,1)} async-done(((bf16[64,1024]{1,0:T(8,128)(2,1)}), bf16[64,1024]{1,0:T(8,128)(2,1)}) %all-reduce.3.cloned.1.call-update) | async-done | bytes 131088 | tf_op jit(solution)/shard_map/while/body/eval_jaxpr/psum | solution.py:89
  338.9 3.9 convolution_convert_fusion.9
  342.7 0.0 all-reduce.5.cloned.1.call-update
  342.8 72.4 %all-reduce.5.cloned.1.call-done = bf16[64,2048]{1,0:T(8,128)(2,1)} async-done(((bf16[64,2048]{1,0:T(8,128)(2,1)}), bf16[64,2048]{1,0:T(8,128)(2,1)}) %all-reduce.5.cloned.1.call-update) | async-done | bytes 262160 | tf_op jit(solution)/shard_map/while/body/eval_jaxpr/psum | solution.py:93
  415.1 1.1 select_dynamic-update-slice_fusion.7
  416.2 1.3 collective-permute-start
  417.5 0.2 select_dynamic-update-slice_fusion.8
  417.7 6.8 %collective-permute-done = bf16[64,2048]{1,0:T(8,128)(2,1)S(1)} collective-permute-done((bf16[64,2048]{1,0:T(8,128)(2,1)S(1)}, bf16[64,2048]{1,0:T(8,128)(2,1)S(1)}, u32[]{:S(2)}, u32[]{:S(2)}) %collective-permute-start) | collective-permute-done | bytes 262176 | tf_op jit(solution)/shard_map/while/body/eval_jaxpr/ppermute | solution.py:45
  424.5 0.7 all-gather.8.cloned.1.call-update
  425.2 0.0 all-gather.10.cloned.1.call-start
  425.3 1.1 fusion.10
  426.4 8.1 %all_gather.18 = bf16[2,128,1024]{2,1,0:T(8,128)(2,1)S(1)} all-gather(bf16[1,128,1024]{2,1,0:T(8,128)(2,1)S(1)} %fusion.10), channel_id=1, replica_groups=mesh['section'=2,'dp'=8,'mp'=2] {'section'}, dimensions={0}, use_global_device_ids=true | all-gather | bytes 786432 | tf_op jit(solution)/shard_map/all_gather | solution.py:123
  434.5 12.7 %all-gather = bf16[256,1024]{1,0:T(8,128)(2,1)S(1)} all-gather(bf16[128,1024]{1,0:T(8,128)(2,1)S(1)} %get-tuple-element.260), channel_id=2, replica_groups=mesh['section'=2,'dp'=8,'mp'=2] {'section'}, dimensions={0}, use_global_device_ids=true | all-gather | bytes 786432 | tf_op jit(solution)/shard_map/all_gather | solution.py:122
  447.2 0.0 all-gather.10.cloned.1.call-update
  447.2 3.3 all-gather.8.cloned.1.call-done
  450.5 1.8 convolution_convert_fusion.5
  452.3 1.8 convolution_convert_fusion.4
  454.1 2.8 add_bitcast_fusion.1
  456.9 15.7 %all-gather.10.cloned.1.call-done = bf16[256,2048]{1,0:T(8,128)(2,1)} async-done(((bf16[128,2048]{1,0:T(8,128)(2,1)}), bf16[256,2048]{1,0:T(8,128)(2,1)}) %all-gather.10.cloned.1.call-update) | async-done | bytes 1048592 | tf_op jit(solution)/shard_map/all_gather | solution.py:121
  472.7 1.8 convolution_convert_fusion.3
  474.4 1.8 convolution_convert_fusion.2
  476.2 2.8 add_bitcast_fusion
  (18 shorter events, 0.2 us)
Async XLA Ops:
  7.2 94.8 %all-gather.6.cloned.1.call-start = ((), (), s32[]{:S(2)}) async-start(), calls=%async_computation | async-start | bytes 6291456 | tf_op jit(solution)/shard_map/all_gather | solution.py:70
  7.9 83.7 %collective-permute-start.1 = (bf16[1,1,1,512,2048]{4,3,2,1,0:T(8,128)(2,1)}, bf16[1,1,1,512,2048]{4,3,2,1,0:T(8,128)(2,1)S(1)}, u32[]{:S(2)}, u32[]{:S(2)}) collective-permute-start(bf16[1,1,1,512,2048]{4,3,2,1,0:T(8,128)(2,1)} %bitcast.39), channel_id=1, source_target_pairs={{0,16},{16,0},{1,17},{17,1},{2,18},{18,2},{3,19},{19,3},{4,20},{20... | collective-permute-start | bytes 6291464 | tf_op jit(solution)/shard_map/ppermute | solution.py:23
  93.5 8.6 %copy-start.2 = (bf16[1,128,1024]{2,1,0:T(8,128)(2,1)S(1)}, bf16[1,128,1024]{2,1,0:T(8,128)(2,1)}, u32[]{:S(2)}) copy-start(bf16[1,128,1024]{2,1,0:T(8,128)(2,1)} %param.8) | copy-start | bytes 786436
  93.5 8.6 %copy-start.4 = (bf16[128,2048]{1,0:T(8,128)(2,1)S(1)}, bf16[128,2048]{1,0:T(8,128)(2,1)}, u32[]{:S(2)}) copy-start(bf16[128,2048]{1,0:T(8,128)(2,1)} %param.9) | copy-start | bytes 1572868
  102.2 24.0 %all-reduce.3.cloned.1.call-start = ((), (), s32[]{:S(2)}) async-start(), calls=%async_computation.3 | async-start | bytes 262144 | tf_op jit(solution)/shard_map/while/body/eval_jaxpr/psum | solution.py:89
  106.6 95.8 %all-reduce.5.cloned.1.call-start = ((), (), s32[]{:S(2)}) async-start(), calls=%async_computation.4 | async-start | bytes 524288 | tf_op jit(solution)/shard_map/while/body/eval_jaxpr/psum | solution.py:93
  126.2 78.6 %copy-start = (bf16[64,1024]{1,0:T(8,128)(2,1)S(1)}, bf16[64,1024]{1,0:T(8,128)(2,1)}, u32[]{:S(2)}) copy-start(bf16[64,1024]{1,0:T(8,128)(2,1)} %all-reduce.3.cloned.1.call-done) | copy-start | bytes 393220 | tf_op jit(solution)/shard_map/while
  203.5 8.3 %collective-permute-start = (bf16[64,2048]{1,0:T(8,128)(2,1)S(1)}, bf16[64,2048]{1,0:T(8,128)(2,1)S(1)}, u32[]{:S(2)}, u32[]{:S(2)}) collective-permute-start(bf16[64,2048]{1,0:T(8,128)(2,1)S(1)} %get-tuple-element.366), channel_id=1, source_target_pairs={{16,0},{17,1},{18,2},{19,3},{20,4},{21,5},{22,6},{23,7},{24,8},{25... | collective-permute-start | bytes 786440 | tf_op jit(solution)/shard_map/while/body/eval_jaxpr/ppermute | solution.py:45
  211.8 20.8 %all-reduce.3.cloned.1.call-start = ((), (), s32[]{:S(2)}) async-start(), calls=%async_computation.3 | async-start | bytes 262144 | tf_op jit(solution)/shard_map/while/body/eval_jaxpr/psum | solution.py:89
  216.2 92.6 %all-reduce.5.cloned.1.call-start = ((), (), s32[]{:S(2)}) async-start(), calls=%async_computation.4 | async-start | bytes 524288 | tf_op jit(solution)/shard_map/while/body/eval_jaxpr/psum | solution.py:93
  232.5 78.6 %copy-start = (bf16[64,1024]{1,0:T(8,128)(2,1)S(1)}, bf16[64,1024]{1,0:T(8,128)(2,1)}, u32[]{:S(2)}) copy-start(bf16[64,1024]{1,0:T(8,128)(2,1)} %all-reduce.3.cloned.1.call-done) | copy-start | bytes 393220 | tf_op jit(solution)/shard_map/while
  309.8 8.3 %collective-permute-start = (bf16[64,2048]{1,0:T(8,128)(2,1)S(1)}, bf16[64,2048]{1,0:T(8,128)(2,1)S(1)}, u32[]{:S(2)}, u32[]{:S(2)}) collective-permute-start(bf16[64,2048]{1,0:T(8,128)(2,1)S(1)} %get-tuple-element.366), channel_id=1, source_target_pairs={{16,0},{17,1},{18,2},{19,3},{20,4},{21,5},{22,6},{23,7},{24,8},{25... | collective-permute-start | bytes 786440 | tf_op jit(solution)/shard_map/while/body/eval_jaxpr/ppermute | solution.py:45
  318.1 20.8 %all-reduce.3.cloned.1.call-start = ((), (), s32[]{:S(2)}) async-start(), calls=%async_computation.3 | async-start | bytes 262144 | tf_op jit(solution)/shard_map/while/body/eval_jaxpr/psum | solution.py:89
  322.5 92.6 %all-reduce.5.cloned.1.call-start = ((), (), s32[]{:S(2)}) async-start(), calls=%async_computation.4 | async-start | bytes 524288 | tf_op jit(solution)/shard_map/while/body/eval_jaxpr/psum | solution.py:93
  338.9 78.6 %copy-start = (bf16[64,1024]{1,0:T(8,128)(2,1)S(1)}, bf16[64,1024]{1,0:T(8,128)(2,1)}, u32[]{:S(2)}) copy-start(bf16[64,1024]{1,0:T(8,128)(2,1)} %all-reduce.3.cloned.1.call-done) | copy-start | bytes 393220 | tf_op jit(solution)/shard_map/while
  416.2 8.3 %collective-permute-start = (bf16[64,2048]{1,0:T(8,128)(2,1)S(1)}, bf16[64,2048]{1,0:T(8,128)(2,1)S(1)}, u32[]{:S(2)}, u32[]{:S(2)}) collective-permute-start(bf16[64,2048]{1,0:T(8,128)(2,1)S(1)} %get-tuple-element.366), channel_id=1, source_target_pairs={{16,0},{17,1},{18,2},{19,3},{20,4},{21,5},{22,6},{23,7},{24,8},{25... | collective-permute-start | bytes 786440 | tf_op jit(solution)/shard_map/while/body/eval_jaxpr/ppermute | solution.py:45
  424.5 22.7 %copy-start.1 = (bf16[128,2048]{1,0:T(8,128)(2,1)}, bf16[128,2048]{1,0:T(8,128)(2,1)S(1)}, u32[]{:S(2)}) copy-start(bf16[128,2048]{1,0:T(8,128)(2,1)S(1)} %get-tuple-element.261) | copy-start | bytes 1572868
  424.5 29.6 %copy-start.3 = (bf16[128,2048]{1,0:T(8,128)(2,1)}, bf16[128,2048]{1,0:T(8,128)(2,1)S(1)}, u32[]{:S(2)}) copy-start(bf16[128,2048]{1,0:T(8,128)(2,1)S(1)} %get-tuple-element.259) | copy-start | bytes 1572868
  424.5 26.1 %all-gather.8.cloned.1.call-start = ((), (), s32[]{:S(2)}) async-start(), calls=%async_computation.1 | async-start | bytes 1572864 | tf_op jit(solution)/shard_map/all_gather | solution.py:120
  425.2 47.5 %all-gather.10.cloned.1.call-start = ((), (), s32[]{:S(2)}) async-start(), calls=%async_computation.2 | async-start | bytes 1572864 | tf_op jit(solution)/shard_map/all_gather | solution.py:121
Sparse Core Ops, SparseCore 0:
  9.5 92.4 all-gather.5
  106.7 19.4 all-reduce.2
  130.2 72.2 all-reduce.4
  216.3 16.1 all-reduce.2
  236.5 72.1 all-reduce.4
  322.6 16.1 all-reduce.2
  342.9 72.2 all-reduce.4
  426.8 23.6 all-gather.7
  452.7 19.9 all-gather.9
